TPU v7x, 32 devices: a whole 2x2x4 slice. The times are simulated.
32 devices in a mesh: groups: 2 (over y), col: 16 (over z, x, core).
Axes of the slice: x: 2, y: 2, z: 4, core: 2. Of those that a mesh axis runs over, the one named last changes fastest.
Arguments:
- fields: bfloat16 [32, 137, 2048], P(('groups', 'col')), parts along dimension 0, may hold values from -6 to 6
- level_count: int32 [2048], replicated, may hold values from 68 to 137
- owner: int32 [16], replicated, may hold values from 0 to 15, as said below
- band_start: int32 [16, 37], replicated, may hold values from 0 to 133
- interp_weights: float32 [16, 37, 4], replicated, may hold values from -3 to 3
Outputs:
- timemajor: bfloat16 [32, 37, 2048], P(('groups', 'col')), parts along dimension 0
- series: bfloat16 [96, 37, 16, 128], P(('groups', 'col')), parts along dimension 0
There are 2 independent parts, one for each index of `groups`. A program takes and returns all parts, laid end to end along the dimension named above; an argument that names none is the same for every part. Nothing has to cross between parts.
Inputs may be any that keep to these rules, and one draw needn't show every extreme that they name: No owner holds more than 3 blocks, and some owner holds exactly 3.
All inputs are finite; a program needn't handle non-finite values.
Results may differ from a plain program's by a relative error of at most 0.0085.
Values may be sent and summed in bfloat16 or wider, within the bound.
A program may use at most 64 MiB of HBM per device.

v0:
```python
import functools

import jax
import jax.numpy as jnp
from jax import lax
from jax.experimental import pallas as pl
from jax.experimental.pallas import tpu as pltpu
from jax.sharding import PartitionSpec as P

LEV = 137
PLEV = 37
BAND = 4
CBLK = 128
MOST = 3
LOW = (LEV // 2 - 1) // 16 * 16
ROWS = -(-MOST * PLEV // 8) * 8
CHUNKS = 4


def loop(count, body):
    if count <= 16:
        for i in range(count):
            body(i)
    else:

        def step(i, carry):
            body(i)
            return carry

        lax.fori_loop(0, count, step, 0)


def partner(me, k, n):
    return (me + k) % n
    other = me
    bit = 1
    while bit < n:
        flip = (k // bit) % 2
        other = other + flip * bit * (1 - 2 * ((me // bit) % 2))
        bit *= 2
    return other


def kernel(n, blocks, fields, counts_in, owner_in, starts_in, weights_in, tm_out, series,
           data, counts, owner, starts, weights, tm, res, stage, packed, arrived, wide, table,
           load_sem, small_sem, out_sem, send_sem, recv_sem):
    me = lax.axis_index("col")
    barrier = pltpu.get_barrier_semaphore()

    def greet(i):
        pl.semaphore_signal(
            barrier, inc=1, device_id={"col": partner(me, n - 1 - i, n)},
            device_id_type=pl.DeviceIdType.MESH,
        )

    loop(n - 1, greet)

    smalls = []
    for i, (src, dst) in enumerate(
        [(owner_in, owner), (counts_in, counts), (starts_in, starts), (weights_in, weights)]
    ):
        small = pltpu.make_async_copy(src, dst, small_sem.at[i])
        small.start()
        smalls.append(small)
    width = data.shape[1] // CHUNKS
    loads = []
    for i in range(CHUNKS):
        span = pl.ds(i * width, width)
        load = pltpu.make_async_copy(fields.at[0, :, span], data.at[:, span], load_sem.at[i])
        load.start()
        loads.append(load)

    smalls[0].wait()

    def find(d):
        seen = jnp.int32(0)
        found = [jnp.int32(blocks)] * MOST

        def look(b, carry):
            seen, found = carry
            hit = owner[b] == d
            found = [jnp.where(hit & (seen == s), b, f) for s, f in enumerate(found)]
            return seen + hit.astype(jnp.int32), found

        if blocks <= 16:
            for b in range(blocks):
                seen, found = look(b, (seen, found))
        else:
            seen, found = lax.fori_loop(0, blocks, look, (seen, found))
        for s in range(MOST):
            table[d * MOST + s] = found[s]

    loop(n, find)

    res[blocks] = jnp.zeros(res.shape[1:], jnp.float32)
    stage[...] = jnp.zeros_like(stage)

    def interpolate(b):
        cols = pl.ds(pl.multiple_of(b * CBLK, CBLK), CBLK)
        count = counts[pl.ds(b, 1), :]
        high = data[LOW:, cols].astype(jnp.float32)
        lev = LOW + lax.broadcasted_iota(jnp.int32, high.shape, 0)
        last = jnp.sum(jnp.where(lev == count - 1, high, 0.0), axis=0, keepdims=True)
        high = jnp.where(lev < count, high, last).astype(jnp.bfloat16)
        filled = jnp.concatenate([data[:LOW, cols], high], axis=0)
        start = starts[pl.ds(b, 1), :]
        offset = lax.broadcasted_iota(jnp.int32, (LEV, PLEV), 0) - start
        matrix = jnp.zeros((LEV, PLEV), jnp.float32)
        for k in range(BAND):
            matrix = jnp.where(offset == k, weights[b, pl.ds(k, 1), :], matrix)
        out = lax.dot_general(
            matrix.astype(jnp.bfloat16), filled, (((0,), (0,)), ((), ())),
            preferred_element_type=jnp.float32,
        )
        res[b, :PLEV] = out
        tm[0, :, cols] = out.astype(jnp.bfloat16)

    for small in smalls[1:]:
        small.wait()
    per = blocks // CHUNKS
    for i in range(CHUNKS):
        loads[i].wait()
        if blocks <= 16:
            for b in range(i * per, (i + 1) * per):
                interpolate(b)
        else:
            def step(b, carry, i=i):
                interpolate(b + i * per)
                return carry

            lax.fori_loop(0, per, step, 0)

    def pack(d):
        for s in range(MOST):
            stage[s * PLEV:(s + 1) * PLEV] = res[table[d * MOST + s], :PLEV]
        return stage[...].astype(jnp.bfloat16)

    tm_copy = pltpu.make_async_copy(tm, tm_out, out_sem.at[0])
    tm_copy.start()

    def copy_to(k):
        d = partner(me, k, n)
        return pltpu.make_async_remote_copy(
            src_ref=packed.at[k], dst_ref=arrived.at[me],
            send_sem=send_sem.at[k], recv_sem=recv_sem.at[me],
            device_id={"col": d}, device_id_type=pl.DeviceIdType.MESH,
        )

    def fill(k):
        packed[k] = pack(partner(me, k, n))

    loop(n, fill)

    def spread(t, rows):
        wide[:, pl.ds(t, 1), :] = rows.astype(jnp.float32)[:, None, :]

    spread(me, packed[0])
    pl.semaphore_wait(barrier, n - 1)

    def order(i):
        return i + 1

    def send(i):
        copy_to(order(i)).start()

    loop(n - 1, send)

    def finish(i):
        k = i + 1
        src = (me + n - k) % n
        pltpu.make_async_remote_copy(
            src_ref=packed.at[k], dst_ref=arrived.at[src],
            send_sem=send_sem.at[k], recv_sem=recv_sem.at[src],
            device_id={"col": src}, device_id_type=pl.DeviceIdType.MESH,
        ).wait_recv()
        spread(src, arrived[src])
        copy_to(k).wait_send()

    loop(n - 1, finish)
    for s in range(MOST):
        series[s] = wide[s * PLEV:(s + 1) * PLEV].astype(jnp.bfloat16)
    tm_copy.wait()


def close(tm, series, tm_out, series_out, sems):
    first = pltpu.make_async_copy(series, series_out, sems.at[0])
    second = pltpu.make_async_copy(tm, tm_out, sems.at[1])
    first.start()
    second.start()
    first.wait()
    second.wait()


def per_device(fields, level_count, owner, band_start, interp_weights):
    n = lax.axis_size("col")
    blocks = owner.shape[0]
    anywhere = pl.BlockSpec(memory_space=pl.ANY)
    cols = blocks * CBLK
    tall = -(-PLEV // 8) * 8
    grant = 2 * cols * (LEV + PLEV + 18) + 4 * CBLK * tall * (blocks + 1) + 2 * n * ROWS * CBLK
    grant += blocks * 12 * CBLK * 4 + (3 << 20)
    vmem = pl.BlockSpec(memory_space=pltpu.VMEM)
    grant += 10 * n * ROWS * CBLK
    timemajor, series = pl.pallas_call(
        functools.partial(kernel, n, blocks),
        out_shape=(
            jax.ShapeDtypeStruct((1, PLEV, cols), jnp.bfloat16),
            jax.ShapeDtypeStruct((MOST, PLEV, n, CBLK), jnp.bfloat16),
        ),
        in_specs=[pl.BlockSpec(memory_space=pltpu.HBM)] * 5,
        out_specs=(anywhere, vmem),
        scratch_shapes=[
            pltpu.VMEM((LEV, cols), jnp.bfloat16),
            pltpu.VMEM((blocks, CBLK), jnp.int32),
            pltpu.SMEM((blocks,), jnp.int32),
            pltpu.VMEM((blocks, PLEV), jnp.int32),
            pltpu.VMEM((blocks, BAND, PLEV), jnp.float32),
            pltpu.VMEM((1, PLEV, cols), jnp.bfloat16),
            pltpu.VMEM((blocks + 1, tall, CBLK), jnp.float32),
            pltpu.VMEM((ROWS, CBLK), jnp.float32),
            pltpu.VMEM((n, ROWS, CBLK), jnp.bfloat16),
            pltpu.VMEM((n, ROWS, CBLK), jnp.bfloat16),
            pltpu.VMEM((ROWS, n, CBLK), jnp.float32),
            pltpu.SMEM((n * MOST,), jnp.int32),
            pltpu.SemaphoreType.DMA((CHUNKS,)),
            pltpu.SemaphoreType.DMA((4,)),
            pltpu.SemaphoreType.DMA((2,)),
            pltpu.SemaphoreType.DMA((n,)),
            pltpu.SemaphoreType.DMA((n,)),
        ],
        compiler_params=pltpu.CompilerParams(
            collective_id=0, has_side_effects=True, vmem_limit_bytes=grant
        ),
    )(
        *[pltpu.with_memory_space_constraint(x, pltpu.HBM) for x in (
            fields, level_count.reshape(blocks, CBLK), owner, band_start,
            jnp.swapaxes(interp_weights, 1, 2),
        )]
    )
    return pl.pallas_call(
        close,
        out_shape=(
            jax.ShapeDtypeStruct((1, PLEV, cols), jnp.bfloat16),
            jax.ShapeDtypeStruct((MOST, PLEV, n, CBLK), jnp.bfloat16),
        ),
        in_specs=[vmem, vmem],
        out_specs=(anywhere, anywhere),
        scratch_shapes=[pltpu.SemaphoreType.DMA((2,))],
        compiler_params=pltpu.CompilerParams(vmem_limit_bytes=3 << 20),
    )(timemajor, series)


def solution(mesh):
    placed = (P(("groups", "col"), None, None), P(), P(), P(), P())
    return jax.shard_map(
        per_device,
        mesh=mesh,
        in_specs=placed,
        out_specs=(P(("groups", "col"), None, None), P(("groups", "col"), None, None, None)),
        check_vma=False,
    )
```

profile of v0, /device:TPU:9, one launch (start us, length us, event | category | flops | bytes accessed | tf_op | source)
XLA Modules:
  0.0 17.9 jit_solution(13022965208054408222)
XLA Ops:
  0.6 16.4 %shard_map.68 = (bf16[1,37,2048]{2,1,0:T(8,128)(2,1)S(1)}, bf16[3,37,16,128]{3,2,1,0:T(8,128)(2,1)S(1)}) custom-call(bf16[1,137,2048]{2,1,0:T(8,128)(2,1)} %fields.1, s32[16,128]{1,0:T(8,128)} %bitcast.3, s32[16]{0:T(128)} %owner_in.1, s32[16,37]{1,0:T(8,128)} %starts_in.1, f32[16,4,37]{2,1,0:T(4,128)} %bitcast.2), custom_call_target="tpu_custom_call" | custom-call | tf_op jit(solution)/shard_map/pallas_call | solution.py:204
  17.0 0.8 %shard_map.69 = (bf16[1,37,2048]{2,1,0:T(8,128)(2,1)}, bf16[3,37,16,128]{3,2,1,0:T(8,128)(2,1)}) custom-call(bf16[1,37,2048]{2,1,0:T(8,128)(2,1)S(1)} %get-tuple-element.4.tm, bf16[3,37,16,128]{3,2,1,0:T(8,128)(2,1)S(1)} %get-tuple-element.5.series), custom_call_target="tpu_custom_call" | custom-call | tf_op jit(solution)/shard_map/pallas_call | solution.py:240
where the time goes:
time: 18 us; the launch traced here: 17.9 us
  Pallas kernels  17.2 us (96%)
  between operations  0.64 us (4%)
    pallas_call x1, Pallas kernels, per_device(): pl.pallas_call(functools.partial(kernel, n, blocks), out_shape=(jax.Shape...  16.4 us
    pallas_call x1, Pallas kernels, per_device(): pl.pallas_call(close, out_shape=(jax.ShapeDtypeStruct((1, PLEV, cols), jn...  0.84 us

commit v1 on v0

v1 whole, which is shorter than its diff:
```python
import functools

import jax
import jax.numpy as jnp
from jax import lax
from jax.experimental import pallas as pl
from jax.experimental.pallas import tpu as pltpu
from jax.sharding import PartitionSpec as P

LEV = 137
PLEV = 37
BAND = 4
CBLK = 128
MOST = 3
TILE = 16
LOW = (LEV // 2 - 1) // TILE * TILE
TALL = -(-LEV // TILE) * TILE
ROWS = -(-MOST * PLEV // TILE) * TILE
CHUNKS = 4
BANDS = 4
SEND = ((2, 1, 0, 3), (2, 3, 1, 0), (0, 1, 2, 3), (0, 2, 3, 1))
OWN = 2
TAKE = ((0, 1, 2, 3), (1, 0, 2, 3), (2, 3, 1, 0), (3, 2, 1, 0))


def loop(first, last, body):
    if last - first <= 16:
        for i in range(first, last):
            body(i)
    else:

        def step(i, carry):
            body(i)
            return carry

        lax.fori_loop(first, last, step, 0)


def choose(table, place, band):
    value = jnp.int32(table[0][place])
    for q in range(1, BANDS):
        value = jnp.where(band == q, jnp.int32(table[q][place]), value)
    return value


def kernel(n, blocks, fields, counts_in, owner_in, starts_in, weights_in, tm, series,
           data, counts, owner, starts, weights, start3, weight3, res, packed, arrived, wide,
           load_sem, small_sem, send_sem, recv_sem, ready):
    me = lax.axis_index("col")
    half = n // 2
    quarter = n // BANDS
    band = me // quarter
    seat = me % quarter
    barrier = pltpu.get_barrier_semaphore()

    smalls = []
    for i, (src, dst) in enumerate(
        [(owner_in, owner), (starts_in, starts), (weights_in, weights), (counts_in, counts)]
    ):
        small = pltpu.make_async_copy(src, dst, small_sem.at[i])
        small.start()
        smalls.append(small)
    width = data.shape[1] // CHUNKS
    loads = []
    for i in range(CHUNKS):
        span = pl.ds(i * width, width)
        load = pltpu.make_async_copy(
            fields.at[0, :, span], data.at[:, span], load_sem.at[i]
        )
        load.start()
        loads.append(load)

    other = (1 - me // half) * half

    def greet(i):
        pl.semaphore_signal(
            barrier, inc=1, device_id={"col": other + (me + i) % half},
            device_id_type=pl.DeviceIdType.MESH,
        )

    loop(0, half, greet)

    res[blocks] = jnp.zeros(res.shape[1:], jnp.bfloat16)
    for small in smalls:
        small.wait()

    start3[...] = jnp.concatenate(
        [starts[...].astype(jnp.float32)] * MOST
        + [jnp.full((blocks, CBLK - MOST * PLEV), -float(CBLK), jnp.float32)], axis=1)
    weight3[...] = jnp.concatenate(
        [weights[...]] * MOST
        + [jnp.zeros((blocks * BAND, CBLK - MOST * PLEV), jnp.float32)], axis=1)

    row = lax.broadcasted_iota(jnp.int32, (TILE, CBLK), 0).astype(jnp.float32).astype(jnp.bfloat16)

    def packed_row(ref, i):
        return jnp.broadcast_to(ref[pl.ds(i, 1), :], (TILE, CBLK)).astype(jnp.bfloat16)

    def interpolate(b):
        cols = pl.ds(pl.multiple_of(b * CBLK, CBLK), CBLK)
        zero = jnp.zeros((TILE, CBLK), jnp.bfloat16)
        count = jnp.broadcast_to(
            counts[pl.ds(b, 1), :].astype(jnp.float32), (TILE, CBLK)).astype(jnp.bfloat16)
        first = packed_row(start3, b)
        terms = [packed_row(weight3, b * BAND + k) for k in range(BAND)]
        filled = [data[:LOW, cols]]
        last = zero
        ends = 0.0
        for i in range(LOW, LEV, TILE):
            size = min(TILE, LEV - i)
            part = jnp.where(row[:size] + float(i + 1) == count[:size], data[i:i + size, cols], zero[:size])
            if size == TILE:
                last = last + part
            else:
                ends = jnp.sum(part.astype(jnp.float32), axis=0, keepdims=True)
        last = jnp.sum(last.astype(jnp.float32), axis=0, keepdims=True) + ends
        last = jnp.broadcast_to(last, (TILE, CBLK)).astype(jnp.bfloat16)
        for i in range(LOW, LEV, TILE):
            size = min(TILE, LEV - i)
            filled.append(jnp.where(row[:size] + float(i) < count[:size], data[i:i + size, cols], last[:size]))
        matrix = []
        for i in range(0, LEV, TILE):
            size = min(TILE, LEV - i)
            offset = (row[:size] + float(i)) - first[:size]
            part = zero[:size]
            for k in range(BAND):
                part = jnp.where(offset == float(k), terms[k][:size], part)
            matrix.append(part)
        out = lax.dot_general(
            jnp.concatenate(matrix, axis=0), jnp.concatenate(filled, axis=0),
            (((0,), (0,)), ((), ())), preferred_element_type=jnp.float32,
        )
        out = out[:ROWS].astype(jnp.bfloat16)
        res[b] = out
        tm[0, :, cols] = out[:PLEV]

    per = blocks // CHUNKS
    for i in range(CHUNKS):
        loads[i].wait()
        loop(i * per, (i + 1) * per, interpolate)

    unit = 1 << blocks.bit_length()

    def find(d):
        def look(i, found):
            b = blocks - 1 - i
            return jnp.where(owner[b] == d, found * unit + b, found)

        found = jnp.int32(blocks)
        for s in range(1, MOST):
            found = found * unit + blocks
        if blocks <= 16:
            for i in range(blocks):
                found = look(i, found)
        else:
            found = lax.fori_loop(0, blocks, look, found)
        return [(found // unit ** s) % unit for s in range(MOST)]

    def pack(k, d):
        where = find(d)
        for i in range(0, ROWS, TILE):
            slots = [s for s in range(MOST) if s * PLEV < i + TILE and (s + 1) * PLEV > i]
            part = res[where[slots[0]], pl.ds(i, TILE)]
            for s in slots[1:]:
                part = jnp.where(
                    row < float(s * PLEV - i), part, res[where[s], pl.ds(i, TILE)])
            packed[k, pl.ds(i, TILE)] = part

    def copy(k, src_dst, slot):
        return pltpu.make_async_remote_copy(
            src_ref=packed.at[k], dst_ref=arrived.at[slot],
            send_sem=send_sem.at[k], recv_sem=recv_sem.at[slot],
            device_id={"col": src_dst}, device_id_type=pl.DeviceIdType.MESH,
        )

    def target(place, j):
        return choose(SEND, place, band) * quarter + (seat + j) % quarter

    def send_band(place):
        def one(j):
            pack(place * quarter + j, target(place, j))

            @pl.when(j > 0)
            def _():
                copy(place * quarter + j - 1, target(place, j - 1), me).start()

        if place != OWN:
            if quarter <= 16:
                for j in range(quarter):
                    pack(place * quarter + j, target(place, j))
                    if j:
                        copy(place * quarter + j - 1, target(place, j - 1), me).start()
            else:
                loop(0, quarter, one)
            copy((place + 1) * quarter - 1, target(place, quarter - 1), me).start()
        else:
            def local(j):
                pack(place * quarter + j, target(place, j))

            loop(0, quarter, local)

            def send(j):
                copy(place * quarter + j, target(place, j), me).start()

            loop(1, quarter, send)

    pl.semaphore_wait(barrier, half)
    pl.semaphore_signal(
        ready, inc=1, device_id={"col": (me + half) % n}, device_id_type=pl.DeviceIdType.MESH)
    send_band(0)
    pl.semaphore_wait(ready, 1)
    for place in range(1, BANDS):
        send_band(place)

    def spread(t, rows):
        wide[:, pl.ds(t, 1), :] = rows.astype(jnp.float32)[:, None, :]

    spread(me, packed[OWN * quarter])

    def take(place):
        def one(j):
            src = choose(TAKE, place, band) * quarter + (seat + quarter - j) % quarter
            copy(0, src, src).wait_recv()
            spread(src, arrived[src])

        loop(1 if place == 0 else 0, quarter, one)

    for place in range(BANDS):
        take(place)
    for s in range(MOST):
        series[s] = wide[s * PLEV:(s + 1) * PLEV].astype(jnp.bfloat16)

    def sent(k):
        copy(k, me, me).wait_send()

    loop(0, OWN * quarter, sent)
    loop(OWN * quarter + 1, n, sent)


def close(tm, series, tm_out, series_out, sems):
    first = pltpu.make_async_copy(series, series_out, sems.at[0])
    second = pltpu.make_async_copy(tm, tm_out, sems.at[1])
    first.start()
    second.start()
    first.wait()
    second.wait()


def per_device(fields, level_count, owner, band_start, interp_weights):
    n = lax.axis_size("col")
    blocks = owner.shape[0]
    anywhere = pl.BlockSpec(memory_space=pl.ANY)
    cols = blocks * CBLK
    vmem = pl.BlockSpec(memory_space=pltpu.VMEM)
    grant = 2 * cols * TALL + 2 * CBLK * ROWS * (blocks + 1 + 2 * n) + 4 * CBLK * n * ROWS
    grant += blocks * CBLK * 4 * 16 + 2 * cols * 48 + 2 * n * ROWS * CBLK + (3 << 20)
    timemajor, series = pl.pallas_call(
        functools.partial(kernel, n, blocks),
        out_shape=(
            jax.ShapeDtypeStruct((1, PLEV, cols), jnp.bfloat16),
            jax.ShapeDtypeStruct((MOST, PLEV, n, CBLK), jnp.bfloat16),
        ),
        in_specs=[pl.BlockSpec(memory_space=pltpu.HBM)] * 5,
        out_specs=(vmem, vmem),
        scratch_shapes=[
            pltpu.VMEM((LEV, cols), jnp.bfloat16),
            pltpu.VMEM((blocks, CBLK), jnp.int32),
            pltpu.SMEM((blocks,), jnp.int32),
            pltpu.VMEM((blocks, PLEV), jnp.int32),
            pltpu.VMEM((blocks * BAND, PLEV), jnp.float32),
            pltpu.VMEM((blocks, CBLK), jnp.float32),
            pltpu.VMEM((blocks * BAND, CBLK), jnp.float32),
            pltpu.VMEM((blocks + 1, ROWS, CBLK), jnp.bfloat16),
            pltpu.VMEM((n, ROWS, CBLK), jnp.bfloat16),
            pltpu.VMEM((n, ROWS, CBLK), jnp.bfloat16),
            pltpu.VMEM((ROWS, n, CBLK), jnp.float32),
            pltpu.SemaphoreType.DMA((CHUNKS,)),
            pltpu.SemaphoreType.DMA((4,)),
            pltpu.SemaphoreType.DMA((n,)),
            pltpu.SemaphoreType.DMA((n,)),
            pltpu.SemaphoreType.REGULAR,
        ],
        compiler_params=pltpu.CompilerParams(
            collective_id=0, has_side_effects=True, vmem_limit_bytes=grant
        ),
    )(
        *[pltpu.with_memory_space_constraint(x, pltpu.HBM) for x in (
            fields, level_count.reshape(blocks, CBLK), owner, band_start,
            jnp.swapaxes(interp_weights, 1, 2).reshape(blocks * BAND, PLEV),
        )]
    )
    return pl.pallas_call(
        close,
        out_shape=(
            jax.ShapeDtypeStruct((1, PLEV, cols), jnp.bfloat16),
            jax.ShapeDtypeStruct((MOST, PLEV, n, CBLK), jnp.bfloat16),
        ),
        in_specs=[vmem, vmem],
        out_specs=(anywhere, anywhere),
        scratch_shapes=[pltpu.SemaphoreType.DMA((2,))],
        compiler_params=pltpu.CompilerParams(vmem_limit_bytes=3 << 20),
    )(timemajor, series)


def solution(mesh):
    placed = (P(("groups", "col"), None, None), P(), P(), P(), P())
    return jax.shard_map(
        per_device,
        mesh=mesh,
        in_specs=placed,
        out_specs=(P(("groups", "col"), None, None), P(("groups", "col"), None, None, None)),
        check_vma=False,
    )
```

time: 18 us -> 17.6 us (0.978)
  Pallas kernels: 17.2 us -> 16.8 us
    pallas_call x1, Pallas kernels: 16.4 us -> 16 us  [per_device(): pl.pallas_call(functools.partial(kernel, n, blocks), out_shape=(jax.Shape...]
where the time goes in v1:
time: 17.6 us; the launch traced here: 17.4 us
  Pallas kernels  16.8 us (95%)
  between operations  0.64 us (4%)
    pallas_call x1, Pallas kernels, per_device(): pl.pallas_call(functools.partial(kernel, n, blocks), out_shape=(jax.Shape...  16 us
    pallas_call x1, Pallas kernels, per_device(): pl.pallas_call(close, out_shape=(jax.ShapeDtypeStruct((1, PLEV, cols), jn...  0.84 us

profile of v1, /device:TPU:9, one launch (start us, length us, event | category | flops | bytes accessed | tf_op | source)
XLA Modules:
  0.0 17.4 jit_solution(2186641024216804426)
XLA Ops:
  0.6 16.0 %shard_map.68 = (bf16[1,37,2048]{2,1,0:T(8,128)(2,1)S(1)}, bf16[3,37,16,128]{3,2,1,0:T(8,128)(2,1)S(1)}) custom-call(bf16[1,137,2048]{2,1,0:T(8,128)(2,1)} %fields.1, s32[16,128]{1,0:T(8,128)} %bitcast.5, s32[16]{0:T(128)} %owner_in.1, s32[16,37]{1,0:T(8,128)} %starts_in.1, f32[64,37]{1,0:T(8,128)} %bitcast.4), custom_call_target="tpu_custom_call" | custom-call | tf_op jit(solution)/shard_map/pallas_call | solution.py:257
  16.6 0.8 %shard_map.69 = (bf16[1,37,2048]{2,1,0:T(8,128)(2,1)}, bf16[3,37,16,128]{3,2,1,0:T(8,128)(2,1)}) custom-call(bf16[1,37,2048]{2,1,0:T(8,128)(2,1)S(1)} %get-tuple-element.4.tm, bf16[3,37,16,128]{3,2,1,0:T(8,128)(2,1)S(1)} %get-tuple-element.5.series), custom_call_target="tpu_custom_call" | custom-call | tf_op jit(solution)/shard_map/pallas_call | solution.py:292

commit v2 on v1

--- a/solution.py
+++ b/solution.py
@@ -16,10 +16,10 @@
 LOW = (LEV // 2 - 1) // TILE * TILE
 TALL = -(-LEV // TILE) * TILE
 ROWS = -(-MOST * PLEV // TILE) * TILE
-CHUNKS = 4
+WIDE = -(-PLEV // TILE) * TILE
 BANDS = 4
-SEND = ((2, 1, 0, 3), (2, 3, 1, 0), (0, 1, 2, 3), (0, 2, 3, 1))
-OWN = 2
+SEND = ((1, 0, 2, 3), (2, 1, 0, 3), (0, 2, 1, 3), (0, 3, 2, 1))
+OWN = 1
 TAKE = ((0, 1, 2, 3), (1, 0, 2, 3), (2, 3, 1, 0), (3, 2, 1, 0))
 
 
@@ -44,8 +44,8 @@
 
 
 def kernel(n, blocks, fields, counts_in, owner_in, starts_in, weights_in, tm, series,
-           data, counts, owner, starts, weights, start3, weight3, res, packed, arrived, wide,
-           load_sem, small_sem, send_sem, recv_sem, ready):
+           data, counts, owner, starts, weights, start_row, weight_row, matrix, res, packed, arrived, wide,
+           load_sem, small_sem, send_sem, recv_sem, near, far):
     me = lax.axis_index("col")
     half = n // 2
     quarter = n // BANDS
@@ -60,49 +60,83 @@
         small = pltpu.make_async_copy(src, dst, small_sem.at[i])
         small.start()
         smalls.append(small)
-    width = data.shape[1] // CHUNKS
-    loads = []
-    for i in range(CHUNKS):
-        span = pl.ds(i * width, width)
-        load = pltpu.make_async_copy(
-            fields.at[0, :, span], data.at[:, span], load_sem.at[i]
-        )
-        load.start()
-        loads.append(load)
-
-    other = (1 - me // half) * half
-
-    def greet(i):
+    load = pltpu.make_async_copy(fields.at[0], data, load_sem)
+    load.start()
+
+    def greet(d):
         pl.semaphore_signal(
-            barrier, inc=1, device_id={"col": other + (me + i) % half},
-            device_id_type=pl.DeviceIdType.MESH,
-        )
-
-    loop(0, half, greet)
+            barrier, inc=1, device_id={"col": d}, device_id_type=pl.DeviceIdType.MESH)
+
+    @pl.when(band < 2)
+    def _():
+        loop(1, n, lambda i: greet((me + i) % n))
+
+    @pl.when(band == 2)
+    def _():
+        loop(0, quarter, lambda i: greet(quarter + i))
+        loop(1, quarter, lambda i: greet(half + (seat + i) % quarter))
+        loop(0, quarter, lambda i: greet(half + quarter + i))
+
+    @pl.when(band == 3)
+    def _():
+        loop(1, quarter, lambda i: greet(half + quarter + (seat + i) % quarter))
 
     res[blocks] = jnp.zeros(res.shape[1:], jnp.bfloat16)
-    for small in smalls:
+    for small in smalls[:-1]:
         small.wait()
 
-    start3[...] = jnp.concatenate(
-        [starts[...].astype(jnp.float32)] * MOST
-        + [jnp.full((blocks, CBLK - MOST * PLEV), -float(CBLK), jnp.float32)], axis=1)
-    weight3[...] = jnp.concatenate(
-        [weights[...]] * MOST
-        + [jnp.zeros((blocks * BAND, CBLK - MOST * PLEV), jnp.float32)], axis=1)
+    start_row[...] = jnp.concatenate(
+        [starts[...].astype(jnp.float32),
+         jnp.full((blocks, CBLK - PLEV), -float(CBLK), jnp.float32)], axis=1)
+    weight_row[...] = jnp.concatenate(
+        [weights[...], jnp.zeros((blocks * BAND, CBLK - PLEV), jnp.float32)], axis=1)
+
+    unit = 1 << blocks.bit_length()
+
+    def find(d):
+        def look(i, found):
+            b = blocks - 1 - i
+            return jnp.where(owner[b] == d, found * unit + b, found)
+
+        found = jnp.int32(blocks)
+        for s in range(1, MOST):
+            found = found * unit + blocks
+        if blocks <= 16:
+            for i in range(blocks):
+                found = look(i, found)
+        else:
+            found = lax.fori_loop(0, blocks, look, found)
+        return [(found // unit ** s) % unit for s in range(MOST)]
+
+    def target(place, j):
+        return choose(SEND, place, band) * quarter + ((seat + j) % quarter if place == OWN else j)
+
+    early = [find(target(0, j)) for j in range(quarter)] if quarter <= 16 else None
 
     row = lax.broadcasted_iota(jnp.int32, (TILE, CBLK), 0).astype(jnp.float32).astype(jnp.bfloat16)
+    zero = jnp.zeros((TILE, CBLK), jnp.bfloat16)
 
     def packed_row(ref, i):
         return jnp.broadcast_to(ref[pl.ds(i, 1), :], (TILE, CBLK)).astype(jnp.bfloat16)
 
+    def build(b):
+        first = packed_row(start_row, b)
+        terms = [packed_row(weight_row, b * BAND + k) for k in range(BAND)]
+        parts = []
+        for i in range(0, TALL, TILE):
+            offset = (row + float(i)) - first
+            part = zero
+            for k in range(BAND):
+                part = jnp.where(offset == float(k), terms[k], part)
+            parts.append(part)
+        matrix[b] = jnp.concatenate(parts, axis=0).T[:WIDE, :LEV]
+
+    loop(0, blocks, build)
+
     def interpolate(b):
         cols = pl.ds(pl.multiple_of(b * CBLK, CBLK), CBLK)
-        zero = jnp.zeros((TILE, CBLK), jnp.bfloat16)
         count = jnp.broadcast_to(
             counts[pl.ds(b, 1), :].astype(jnp.float32), (TILE, CBLK)).astype(jnp.bfloat16)
-        first = packed_row(start3, b)
-        terms = [packed_row(weight3, b * BAND + k) for k in range(BAND)]
         filled = [data[:LOW, cols]]
         last = zero
         ends = 0.0
@@ -118,46 +152,20 @@
         for i in range(LOW, LEV, TILE):
             size = min(TILE, LEV - i)
             filled.append(jnp.where(row[:size] + float(i) < count[:size], data[i:i + size, cols], last[:size]))
-        matrix = []
-        for i in range(0, LEV, TILE):
-            size = min(TILE, LEV - i)
-            offset = (row[:size] + float(i)) - first[:size]
-            part = zero[:size]
-            for k in range(BAND):
-                part = jnp.where(offset == float(k), terms[k][:size], part)
-            matrix.append(part)
-        out = lax.dot_general(
-            jnp.concatenate(matrix, axis=0), jnp.concatenate(filled, axis=0),
-            (((0,), (0,)), ((), ())), preferred_element_type=jnp.float32,
-        )
-        out = out[:ROWS].astype(jnp.bfloat16)
-        res[b] = out
-        tm[0, :, cols] = out[:PLEV]
-
-    per = blocks // CHUNKS
-    for i in range(CHUNKS):
-        loads[i].wait()
-        loop(i * per, (i + 1) * per, interpolate)
-
-    unit = 1 << blocks.bit_length()
-
-    def find(d):
-        def look(i, found):
-            b = blocks - 1 - i
-            return jnp.where(owner[b] == d, found * unit + b, found)
-
-        found = jnp.int32(blocks)
-        for s in range(1, MOST):
-            found = found * unit + blocks
-        if blocks <= 16:
-            for i in range(blocks):
-                found = look(i, found)
-        else:
-            found = lax.fori_loop(0, blocks, look, found)
-        return [(found // unit ** s) % unit for s in range(MOST)]
-
-    def pack(k, d):
-        where = find(d)
+        out = jnp.dot(
+            matrix[b], jnp.concatenate(filled, axis=0), preferred_element_type=jnp.float32)[:PLEV]
+        tm[0, :, cols] = out.astype(jnp.bfloat16)
+        res[b] = jnp.concatenate(
+            [out] * MOST + [jnp.zeros((ROWS - MOST * PLEV, CBLK), jnp.float32)], axis=0,
+        ).astype(jnp.bfloat16)
+
+    for small in smalls[-1:]:
+        small.wait()
+    load.wait()
+    loop(0, blocks, interpolate)
+
+    def pack(k, d, where=None):
+        where = find(d) if where is None else where
         for i in range(0, ROWS, TILE):
             slots = [s for s in range(MOST) if s * PLEV < i + TILE and (s + 1) * PLEV > i]
             part = res[where[slots[0]], pl.ds(i, TILE)]
@@ -173,9 +181,6 @@
             device_id={"col": src_dst}, device_id_type=pl.DeviceIdType.MESH,
         )
 
-    def target(place, j):
-        return choose(SEND, place, band) * quarter + (seat + j) % quarter
-
     def send_band(place):
         def one(j):
             pack(place * quarter + j, target(place, j))
@@ -187,7 +192,7 @@
         if place != OWN:
             if quarter <= 16:
                 for j in range(quarter):
-                    pack(place * quarter + j, target(place, j))
+                    pack(place * quarter + j, target(place, j), None if place else early[j])
                     if j:
                         copy(place * quarter + j - 1, target(place, j - 1), me).start()
             else:
@@ -204,13 +209,34 @@
 
             loop(1, quarter, send)
 
-    pl.semaphore_wait(barrier, half)
-    pl.semaphore_signal(
-        ready, inc=1, device_id={"col": (me + half) % n}, device_id_type=pl.DeviceIdType.MESH)
+    def tell(semaphore, d):
+        pl.semaphore_signal(
+            semaphore, inc=1, device_id={"col": d}, device_id_type=pl.DeviceIdType.MESH)
+
+    for q in range(BANDS):
+        @pl.when(band == q)
+        def _(q=q):
+            pl.semaphore_wait(barrier, (2, 3, 3, 4)[q] * quarter - 1)
+            if q == 1:
+                tell(near, me - quarter)
+            if q == 3:
+                for away in range(1, BANDS):
+                    tell(far, me - away * quarter)
+
     send_band(0)
-    pl.semaphore_wait(ready, 1)
-    for place in range(1, BANDS):
-        send_band(place)
+    send_band(1)
+
+    @pl.when(band == 0)
+    def _():
+        pl.semaphore_wait(near, 1)
+
+    send_band(2)
+
+    @pl.when(band < 3)
+    def _():
+        pl.semaphore_wait(far, 1)
+
+    send_band(3)
 
     def spread(t, rows):
         wide[:, pl.ds(t, 1), :] = rows.astype(jnp.float32)[:, None, :]
@@ -219,7 +245,7 @@
 
     def take(place):
         def one(j):
-            src = choose(TAKE, place, band) * quarter + (seat + quarter - j) % quarter
+            src = choose(TAKE, place, band) * quarter + ((seat + quarter - j) % quarter if place == 0 else j)
             copy(0, src, src).wait_recv()
             spread(src, arrived[src])
 
@@ -253,7 +279,7 @@
     cols = blocks * CBLK
     vmem = pl.BlockSpec(memory_space=pltpu.VMEM)
     grant = 2 * cols * TALL + 2 * CBLK * ROWS * (blocks + 1 + 2 * n) + 4 * CBLK * n * ROWS
-    grant += blocks * CBLK * 4 * 16 + 2 * cols * 48 + 2 * n * ROWS * CBLK + (3 << 20)
+    grant += blocks * CBLK * 4 * 16 + 2 * cols * 48 + 2 * n * ROWS * CBLK + blocks * WIDE * 512 + (3 << 20)
     timemajor, series = pl.pallas_call(
         functools.partial(kernel, n, blocks),
         out_shape=(
@@ -270,14 +296,16 @@
             pltpu.VMEM((blocks * BAND, PLEV), jnp.float32),
             pltpu.VMEM((blocks, CBLK), jnp.float32),
             pltpu.VMEM((blocks * BAND, CBLK), jnp.float32),
+            pltpu.VMEM((blocks, WIDE, LEV), jnp.bfloat16),
             pltpu.VMEM((blocks + 1, ROWS, CBLK), jnp.bfloat16),
             pltpu.VMEM((n, ROWS, CBLK), jnp.bfloat16),
             pltpu.VMEM((n, ROWS, CBLK), jnp.bfloat16),
             pltpu.VMEM((ROWS, n, CBLK), jnp.float32),
-            pltpu.SemaphoreType.DMA((CHUNKS,)),
+            pltpu.SemaphoreType.DMA,
             pltpu.SemaphoreType.DMA((4,)),
             pltpu.SemaphoreType.DMA((n,)),
             pltpu.SemaphoreType.DMA((n,)),
+            pltpu.SemaphoreType.REGULAR,
             pltpu.SemaphoreType.REGULAR,
         ],
         compiler_params=pltpu.CompilerParams(

time: 17.6 us -> 16.4 us (0.932)
  Pallas kernels: 16.8 us -> 15.5 us
    pallas_call x1, Pallas kernels: 16 us -> 14.6 us  [per_device(): pl.pallas_call(functools.partial(kernel, n, blocks), out_shape=(jax.Shape...]
where the time goes in v2:
time: 16.4 us; the launch traced here: 16.1 us
  Pallas kernels  15.5 us (95%)
  between operations  0.64 us (4%)
    pallas_call x1, Pallas kernels, per_device(): pl.pallas_call(functools.partial(kernel, n, blocks), out_shape=(jax.Shape...  14.6 us
    pallas_call x1, Pallas kernels, per_device(): pl.pallas_call(close, out_shape=(jax.ShapeDtypeStruct((1, PLEV, cols), jn...  0.84 us

profile of v2, /device:TPU:9, one launch (start us, length us, event | category | flops | bytes accessed | tf_op | source)
XLA Modules:
  0.0 16.1 jit_solution(5888545363845349731)
XLA Ops:
  0.6 14.6 %shard_map.68 = (bf16[1,37,2048]{2,1,0:T(8,128)(2,1)S(1)}, bf16[3,37,16,128]{3,2,1,0:T(8,128)(2,1)S(1)}) custom-call(bf16[1,137,2048]{2,1,0:T(8,128)(2,1)} %fields.1, s32[16,128]{1,0:T(8,128)} %bitcast.5, s32[16]{0:T(128)} %owner_in.1, s32[16,37]{1,0:T(8,128)} %starts_in.1, f32[64,37]{1,0:T(8,128)} %bitcast.4), custom_call_target="tpu_custom_call" | custom-call | tf_op jit(solution)/shard_map/pallas_call | solution.py:283
  15.3 0.8 %shard_map.69 = (bf16[1,37,2048]{2,1,0:T(8,128)(2,1)}, bf16[3,37,16,128]{3,2,1,0:T(8,128)(2,1)}) custom-call(bf16[1,37,2048]{2,1,0:T(8,128)(2,1)S(1)} %get-tuple-element.4.tm, bf16[3,37,16,128]{3,2,1,0:T(8,128)(2,1)S(1)} %get-tuple-element.5.series), custom_call_target="tpu_custom_call" | custom-call | tf_op jit(solution)/shard_map/pallas_call | solution.py:320

commit v3 on v2

--- a/solution.py
+++ b/solution.py
@@ -18,9 +18,18 @@
 ROWS = -(-MOST * PLEV // TILE) * TILE
 WIDE = -(-PLEV // TILE) * TILE
 BANDS = 4
-SEND = ((1, 0, 2, 3), (2, 1, 0, 3), (0, 2, 1, 3), (0, 3, 2, 1))
-OWN = 1
-TAKE = ((0, 1, 2, 3), (1, 0, 2, 3), (2, 3, 1, 0), (3, 2, 1, 0))
+SEND = ((1, 2, 0, 3), (2, 0, 1, 3), (0, 1, 2, 3), (0, 2, 3, 1))
+OWN = 2
+OWN_AT = 1
+CUTS = (0, 16)
+EARLY = 2
+STAGES = (0, 2, 4, 1 << 20)
+STEPS = len(STAGES) - 1
+EDGE = ((1, 0, 2, 3), (2, 3, 0, 1))
+EDGE_TAKE = ((0, 1, 3, 2), (3, 2, 0, 1))
+CROSS = (((3, 0), (3, 1), (3, 2), (3, 3), (2, 0), (2, 1), (2, 2), (2, 3)),
+         ((0, 0), (0, 1), (0, 2), (0, 3), (1, 0), (1, 1), (1, 2), (1, 3)))
+TAKE = ((0, 3, 2, 1), (1, 0, 3, 2), (2, 3, 0, 1), (3, 2, 0, 1))
 
 
 def loop(first, last, body):
@@ -45,7 +54,7 @@
 
 def kernel(n, blocks, fields, counts_in, owner_in, starts_in, weights_in, tm, series,
            data, counts, owner, starts, weights, start_row, weight_row, matrix, res, packed, arrived, wide,
-           load_sem, small_sem, send_sem, recv_sem, near, far):
+           load_sem, small_sem, send_sem, recv_sem, near, far, queued, again, queue_sem, again_sem, *lists):
     me = lax.axis_index("col")
     half = n // 2
     quarter = n // BANDS
@@ -60,8 +69,12 @@
         small = pltpu.make_async_copy(src, dst, small_sem.at[i])
         small.start()
         smalls.append(small)
-    load = pltpu.make_async_copy(fields.at[0], data, load_sem)
-    load.start()
+    loads = []
+    for i, (first, last) in enumerate(zip(CUTS, CUTS[1:])):
+        span = pl.ds(blocks * first // 16 * CBLK, blocks * (last - first) // 16 * CBLK)
+        load = pltpu.make_async_copy(fields.at[0, :, span], data.at[:, span], load_sem.at[i])
+        load.start()
+        loads.append(load)
 
     def greet(d):
         pl.semaphore_signal(
@@ -74,7 +87,6 @@
     @pl.when(band == 2)
     def _():
         loop(0, quarter, lambda i: greet(quarter + i))
-        loop(1, quarter, lambda i: greet(half + (seat + i) % quarter))
         loop(0, quarter, lambda i: greet(half + quarter + i))
 
     @pl.when(band == 3)
@@ -82,6 +94,8 @@
         loop(1, quarter, lambda i: greet(half + quarter + (seat + i) % quarter))
 
     res[blocks] = jnp.zeros(res.shape[1:], jnp.bfloat16)
+    for part in lists:
+        part[part.shape[0] - 1] = jnp.zeros(part.shape[1:], jnp.bfloat16)
     for small in smalls[:-1]:
         small.wait()
 
@@ -92,6 +106,27 @@
         [weights[...], jnp.zeros((blocks * BAND, CBLK - PLEV), jnp.float32)], axis=1)
 
     unit = 1 << blocks.bit_length()
+    relayed = blocks <= 16 and quarter <= 16
+    groups = -(-blocks // MOST)
+
+    def third(x):
+        return (x * 43) >> 7
+
+    def shift(c, turn):
+        return jnp.where(c + turn >= MOST, c + turn - MOST, c + turn)
+
+    if relayed:
+        lower = jnp.int32(0)
+        for b in range(blocks):
+            lower = lower + jnp.where(owner[b] < half, 1, 0)
+
+    def before(d):
+        if not relayed:
+            return jnp.int32(0)
+        count = jnp.int32(0)
+        for b in range(blocks):
+            count = count + jnp.where(owner[b] < d, 1, 0)
+        return count - jnp.where(d >= half, lower, 0)
 
     def find(d):
         def look(i, found):
@@ -106,12 +141,58 @@
                 found = look(i, found)
         else:
             found = lax.fori_loop(0, blocks, look, found)
-        return [(found // unit ** s) % unit for s in range(MOST)]
+        found = [(found // unit ** s) % unit for s in range(MOST)]
+        if relayed:
+            first = before(d)
+            turn = first - MOST * third(first)
+            found = [
+                jnp.where(turn == 0, found[c], jnp.where(turn == 1, found[(c + 2) % 3], found[(c + 1) % 3]))
+                for c in range(MOST)
+            ]
+        return found
+
+    def locate(d):
+        first = before(d)
+        last = first
+        for b in range(blocks):
+            last = last + jnp.where(owner[b] == d, 1, 0)
+        turn = first - MOST * third(first)
+        where = []
+        for c in range(MOST):
+            place = first + jnp.where(c >= turn, c - turn, c - turn + MOST)
+            where.append(jnp.where(place < last, third(place), groups))
+        return where
+
+    def ordered(base):
+        keys = []
+        for b in range(blocks):
+            away = owner[b] - base
+            keys.append(jnp.where(away < 0, away + n, away) * unit + b)
+        size = 1 << (blocks - 1).bit_length()
+        keys += [jnp.int32(n * unit + blocks)] * (size - blocks)
+        p = 1
+        while p < size:
+            k = p
+            while k >= 1:
+                for j in range(k % p, size - k, 2 * k):
+                    for i in range(min(k, size - j - k)):
+                        if (i + j) // (2 * p) == (i + j + k) // (2 * p):
+                            x, y = keys[i + j], keys[i + j + k]
+                            keys[i + j], keys[i + j + k] = jnp.minimum(x, y), jnp.maximum(x, y)
+                k //= 2
+            p *= 2
+        keys = [key % unit for key in keys[:blocks]]
+        return keys + [jnp.int32(blocks)] * (groups * MOST - blocks)
 
     def target(place, j):
         return choose(SEND, place, band) * quarter + ((seat + j) % quarter if place == OWN else j)
 
-    early = [find(target(0, j)) for j in range(quarter)] if quarter <= 16 else None
+    early = None
+    if relayed:
+        queue = ordered((1 - me // half) * half)
+        inner = (band == 1) | (band == 2)
+    elif quarter <= 16:
+        early = [find(target(0, j)) for j in range(quarter)]
 
     row = lax.broadcasted_iota(jnp.int32, (TILE, CBLK), 0).astype(jnp.float32).astype(jnp.bfloat16)
     zero = jnp.zeros((TILE, CBLK), jnp.bfloat16)
@@ -161,23 +242,26 @@
 
     for small in smalls[-1:]:
         small.wait()
-    load.wait()
-    loop(0, blocks, interpolate)
-
-    def pack(k, d, where=None):
-        where = find(d) if where is None else where
-        for i in range(0, ROWS, TILE):
+    for load, first, last in zip(loads, CUTS, CUTS[1:]):
+        load.wait()
+        loop(blocks * first // 16, blocks * last // 16, interpolate)
+
+    def fill(target, source, where, rows=ROWS):
+        for i in range(0, rows, TILE):
             slots = [s for s in range(MOST) if s * PLEV < i + TILE and (s + 1) * PLEV > i]
-            part = res[where[slots[0]], pl.ds(i, TILE)]
+            part = source[where[slots[0]], pl.ds(i, TILE)]
             for s in slots[1:]:
                 part = jnp.where(
-                    row < float(s * PLEV - i), part, res[where[s], pl.ds(i, TILE)])
-            packed[k, pl.ds(i, TILE)] = part
-
-    def copy(k, src_dst, slot):
+                    row < float(s * PLEV - i), part, source[where[s], pl.ds(i, TILE)])
+            target[pl.ds(i, TILE)] = part
+
+    def pack(k, d, where=None):
+        fill(packed.at[k], res, find(d) if where is None else where)
+
+    def copy(k, src_dst, slot, source=None, sems=None):
         return pltpu.make_async_remote_copy(
-            src_ref=packed.at[k], dst_ref=arrived.at[slot],
-            send_sem=send_sem.at[k], recv_sem=recv_sem.at[slot],
+            src_ref=(packed if source is None else source).at[k], dst_ref=arrived.at[slot],
+            send_sem=(send_sem if sems is None else sems).at[k], recv_sem=recv_sem.at[slot],
             device_id={"col": src_dst}, device_id_type=pl.DeviceIdType.MESH,
         )
 
@@ -216,51 +300,219 @@
     for q in range(BANDS):
         @pl.when(band == q)
         def _(q=q):
-            pl.semaphore_wait(barrier, (2, 3, 3, 4)[q] * quarter - 1)
+            pl.semaphore_wait(barrier, (2 * quarter - 1, 3 * quarter - 1, half, n - 1)[q])
             if q == 1:
                 tell(near, me - quarter)
+                tell(near, me + quarter)
             if q == 3:
                 for away in range(1, BANDS):
-                    tell(far, me - away * quarter)
-
-    send_band(0)
-    send_band(1)
-
-    @pl.when(band == 0)
-    def _():
-        pl.semaphore_wait(near, 1)
-
-    send_band(2)
-
-    @pl.when(band < 3)
-    def _():
-        pl.semaphore_wait(far, 1)
-
-    send_band(3)
+                    if not (relayed and away == 2):
+                        tell(far, me - away * quarter)
 
     def spread(t, rows):
         wide[:, pl.ds(t, 1), :] = rows.astype(jnp.float32)[:, None, :]
 
-    spread(me, packed[OWN * quarter])
-
-    def take(place):
-        def one(j):
-            src = choose(TAKE, place, band) * quarter + ((seat + quarter - j) % quarter if place == 0 else j)
-            copy(0, src, src).wait_recv()
-            spread(src, arrived[src])
-
-        loop(1 if place == 0 else 0, quarter, one)
-
-    for place in range(BANDS):
-        take(place)
+    def burst(count, pack_one, copy_one):
+        for i in range(count):
+            pack_one(i)
+            if i:
+                copy_one(i - 1).start()
+        copy_one(count - 1).start()
+
+    def own_band(first):
+        peer = [band * quarter + (seat + j) % quarter for j in range(quarter)]
+        for j in range(quarter):
+            pack(first + j, peer[j])
+        for j in range(1, quarter):
+            copy(first + j, peer[j], me).start()
+
+    def send_to(first, dest):
+        burst(quarter, lambda j: pack(first + j, dest * quarter + j),
+              lambda j: copy(first + j, dest * quarter + j, me))
+
+    def take_from(src):
+        copy(0, src, src).wait_recv()
+        spread(src, arrived[src])
+
+    def take_own():
+        for j in range(1, quarter):
+            take_from(band * quarter + (seat + j) % quarter)
+
+    def sent(k, source=None, sems=None):
+        copy(k, me, me, source, sems).wait_send()
+
+    if relayed:
+        tail = -(-(blocks - MOST * (groups - 1)) * PLEV // TILE) * TILE
+        mirror = jnp.where(band == 1, me + quarter, me - quarter)
+
+        def stage_copies(t):
+            first, last = STAGES[t], min(STAGES[t + 1], groups)
+            spans = [pl.ds(first, last - first)] if last < groups else [
+                pl.ds(first, last - 1 - first), (groups - 1, pl.ds(0, tail))]
+            return [
+                pltpu.make_async_remote_copy(
+                    src_ref=queued.at[span], dst_ref=lists[t].at[span],
+                    send_sem=queue_sem.at[2 * t + i], recv_sem=queue_sem.at[2 * STEPS + 2 * t + i],
+                    device_id={"col": mirror}, device_id_type=pl.DeviceIdType.MESH)
+                for i, span in enumerate(spans)
+            ]
+
+        def local(j):
+            return copy(j, quarter + j, me)
+
+        @pl.when(band == 0)
+        def _():
+            for j in range(quarter):
+                pack(j, quarter + j)
+                if 0 < j <= EARLY:
+                    local(j - 1).start()
+
+        @pl.when(band == 3)
+        def _():
+            send_to(0, EDGE[1][0])
+
+        @pl.when(inner)
+        def _():
+            for g in range(groups):
+                fill(queued.at[g], res, queue[MOST * g:MOST * g + MOST],
+                     ROWS if g < groups - 1 else tail)
+                for t in range(STEPS - 1):
+                    if g == STAGES[t + 1]:
+                        for c in stage_copies(t):
+                            c.start()
+            for c in stage_copies(STEPS - 1):
+                c.start()
+
+            @pl.when(band == 2)
+            def _():
+                pl.semaphore_wait(near, 1)
+                pl.semaphore_wait(far, 1)
+
+            send_to(0, jnp.where(band == 1, 0, 3))
+
+        own_band(OWN_AT * quarter)
+        spread(me, packed[OWN_AT * quarter])
+
+        def take_edge(place, j):
+            take_from(jnp.where(band == 0, EDGE_TAKE[0][place], EDGE_TAKE[1][place]) * quarter + j)
+
+        @pl.when(band == 0)
+        def _():
+            pl.semaphore_wait(near, 1)
+            pl.semaphore_wait(far, 1)
+            for j in range(EARLY, quarter):
+                local(j).start()
+
+        @pl.when(jnp.logical_not(inner))
+        def _():
+            cross = [jnp.where(band == 0, p * quarter + a, q * quarter + b)
+                     for (p, a), (q, b) in zip(*[
+                         [(p, a * quarter // 4 + i) for p, a in order for i in range(quarter // 4)]
+                         for order in CROSS])]
+            burst(half, lambda i: pack(half + i, cross[i]), lambda i: copy(half + i, cross[i], me))
+            take_own()
+
+            for place in range(1, BANDS):
+                for j in range(quarter):
+                    take_edge(place, j)
+            for k in range(2 * quarter, 4 * quarter):
+                sent(k)
+
+        @pl.when(inner)
+        def _():
+            outer = jnp.where(band == 1, 0, 3)
+            peers = [outer * quarter + j for j in range(quarter)]
+            peers += [band * quarter + (seat + j) % quarter for j in range(1, quarter)]
+            peers += [me]
+            where = [locate(d) for d in peers]
+            def pass_on(i):
+                return copy(i, peers[i], mirror, again, again_sem)
+
+            for t in range(STEPS):
+                for c in stage_copies(t):
+                    c.wait_recv()
+                for g in range(STAGES[t]):
+                    lists[t][g] = lists[t - 1][g]
+                if t < STEPS - 1:
+                    @pl.when(band == 1)
+                    def _(t=t):
+                        for i in range(STAGES[t], STAGES[t + 1]):
+                            fill(again.at[i], lists[t], [
+                                jnp.where(w == groups, STAGES[t + 1], w) for w in where[i]])
+                        for i in range(STAGES[t], STAGES[t + 1]):
+                            pass_on(i).start()
+
+            @pl.when(band == 2)
+            def _():
+                for i in range(STAGES[STEPS - 1]):
+                    fill(again.at[i], lists[STEPS - 1], where[i])
+                    if i:
+                        pass_on(i - 1).start()
+                pass_on(STAGES[STEPS - 1] - 1).start()
+
+            for i in range(STAGES[STEPS - 1], half):
+                fill(again.at[i], lists[STEPS - 1], where[i])
+                if i > STAGES[STEPS - 1]:
+                    pass_on(i - 1).start()
+            take_own()
+            for j in range(quarter):
+                take_from(outer * quarter + j)
+            spread(mirror, again[half - 1])
+            for j in range(1, quarter):
+                take_from((BANDS - 1 - band) * quarter + (seat + j) % quarter)
+            for j in range(quarter):
+                take_from((BANDS - 1 - outer) * quarter + j)
+            for t in range(STEPS):
+                for c in stage_copies(t):
+                    c.wait_send()
+            for i in range(half - 1):
+                sent(i, again, again_sem)
+
+        for k in range(quarter):
+            sent(k)
+        for k in range(OWN_AT * quarter + 1, (OWN_AT + 1) * quarter):
+            sent(k)
+    else:
+        send_band(0)
+
+        @pl.when(band == 0)
+        def _():
+            pl.semaphore_wait(near, 1)
+
+        send_band(1)
+
+        @pl.when(band == 2)
+        def _():
+            pl.semaphore_wait(near, 1)
+
+        send_band(2)
+
+        @pl.when(band < 3)
+        def _():
+            pl.semaphore_wait(far, 1)
+
+        send_band(3)
+
+        spread(me, packed[OWN * quarter])
+
+        def take(place):
+            def one(j):
+                src = choose(TAKE, place, band) * quarter + ((seat + quarter - j) % quarter if place == 0 else j)
+                copy(0, src, src).wait_recv()
+                spread(src, arrived[src])
+
+            loop(1 if place == 0 else 0, quarter, one)
+
+        for place in range(BANDS):
+            take(place)
+
+        loop(0, OWN * quarter, sent)
+        loop(OWN * quarter + 1, n, sent)
+
+    turn = before(me)
+    turn = turn - MOST * third(turn)
     for s in range(MOST):
-        series[s] = wide[s * PLEV:(s + 1) * PLEV].astype(jnp.bfloat16)
-
-    def sent(k):
-        copy(k, me, me).wait_send()
-
-    loop(0, OWN * quarter, sent)
-    loop(OWN * quarter + 1, n, sent)
+        series[s] = wide[pl.ds(shift(s, turn) * PLEV, PLEV)].astype(jnp.bfloat16)
 
 
 def close(tm, series, tm_out, series_out, sems):
@@ -280,6 +532,7 @@
     vmem = pl.BlockSpec(memory_space=pltpu.VMEM)
     grant = 2 * cols * TALL + 2 * CBLK * ROWS * (blocks + 1 + 2 * n) + 4 * CBLK * n * ROWS
     grant += blocks * CBLK * 4 * 16 + 2 * cols * 48 + 2 * n * ROWS * CBLK + blocks * WIDE * 512 + (3 << 20)
+    grant += 2 * (blocks + n) * ROWS * CBLK
     timemajor, series = pl.pallas_call(
         functools.partial(kernel, n, blocks),
         out_shape=(
@@ -301,12 +554,17 @@
             pltpu.VMEM((n, ROWS, CBLK), jnp.bfloat16),
             pltpu.VMEM((n, ROWS, CBLK), jnp.bfloat16),
             pltpu.VMEM((ROWS, n, CBLK), jnp.float32),
-            pltpu.SemaphoreType.DMA,
+            pltpu.SemaphoreType.DMA((len(CUTS) - 1,)),
             pltpu.SemaphoreType.DMA((4,)),
             pltpu.SemaphoreType.DMA((n,)),
             pltpu.SemaphoreType.DMA((n,)),
             pltpu.SemaphoreType.REGULAR,
             pltpu.SemaphoreType.REGULAR,
+            pltpu.VMEM((-(-blocks // MOST), ROWS, CBLK), jnp.bfloat16),
+            pltpu.VMEM((n // 2, ROWS, CBLK), jnp.bfloat16),
+            pltpu.SemaphoreType.DMA((4 * STEPS,)),
+            pltpu.SemaphoreType.DMA((n // 2,)),
+            *[pltpu.VMEM((min(last, -(-blocks // MOST)) + 1, ROWS, CBLK), jnp.bfloat16) for last in STAGES[1:]],
         ],
         compiler_params=pltpu.CompilerParams(
             collective_id=0, has_side_effects=True, vmem_limit_bytes=grant

time: 16.4 us -> 15.3 us (0.933)
  the two profiles are of different devices: /device:TPU:9 before, /device:TPU:0 now
where the time goes in v3:
time: 15.3 us; the launch traced here: 15.2 us
  Pallas kernels  14.5 us (95%)
  between operations  0.64 us (4%)
    pallas_call x1, Pallas kernels, per_device(): pl.pallas_call(functools.partial(kernel, n, blocks), out_shape=(jax.Shape...  13.7 us
    pallas_call x1, Pallas kernels, per_device(): pl.pallas_call(close, out_shape=(jax.ShapeDtypeStruct((1, PLEV, cols), jn...  0.84 us

profile of v3, /device:TPU:0, one launch (start us, length us, event | category | flops | bytes accessed | tf_op | source)
XLA Modules:
  0.0 15.2 jit_solution(7188520553906206075)
XLA Ops:
  0.6 13.7 %shard_map.68 = (bf16[1,37,2048]{2,1,0:T(8,128)(2,1)S(1)}, bf16[3,37,16,128]{3,2,1,0:T(8,128)(2,1)S(1)}) custom-call(bf16[1,137,2048]{2,1,0:T(8,128)(2,1)} %fields.1, s32[16,128]{1,0:T(8,128)} %bitcast.5, s32[16]{0:T(128)} %owner_in.1, s32[16,37]{1,0:T(8,128)} %starts_in.1, f32[64,37]{1,0:T(8,128)} %bitcast.4), custom_call_target="tpu_custom_call" | custom-call | tf_op jit(solution)/shard_map/pallas_call | solution.py:536
  14.3 0.8 %shard_map.69 = (bf16[1,37,2048]{2,1,0:T(8,128)(2,1)}, bf16[3,37,16,128]{3,2,1,0:T(8,128)(2,1)}) custom-call(bf16[1,37,2048]{2,1,0:T(8,128)(2,1)S(1)} %get-tuple-element.4.tm, bf16[3,37,16,128]{3,2,1,0:T(8,128)(2,1)S(1)} %get-tuple-element.5.series), custom_call_target="tpu_custom_call" | custom-call | tf_op jit(solution)/shard_map/pallas_call | solution.py:578

commit v4 on v3

--- a/solution.py
+++ b/solution.py
@@ -18,18 +18,17 @@
 ROWS = -(-MOST * PLEV // TILE) * TILE
 WIDE = -(-PLEV // TILE) * TILE
 BANDS = 4
+CUTS = (0, 16)
 SEND = ((1, 2, 0, 3), (2, 0, 1, 3), (0, 1, 2, 3), (0, 2, 3, 1))
 OWN = 2
+TAKE = ((0, 3, 2, 1), (1, 0, 3, 2), (2, 3, 0, 1), (3, 2, 0, 1))
 OWN_AT = 1
-CUTS = (0, 16)
-EARLY = 2
+EARLY = (4, 3)
+CROSS = (((3, 0), (3, 1), (3, 2), (3, 3), (2, 0), (2, 1), (2, 2), (2, 3)),
+         ((2, 0), (2, 1), (2, 2), (0, 0), (2, 3), (0, 1), (0, 2), (1, 0), (0, 3), (1, 1), (1, 2), (1, 3)))
+EDGE_TAKE = ((0, 1, 3, 2), (3, 2, 0, 1))
 STAGES = (0, 2, 4, 1 << 20)
 STEPS = len(STAGES) - 1
-EDGE = ((1, 0, 2, 3), (2, 3, 0, 1))
-EDGE_TAKE = ((0, 1, 3, 2), (3, 2, 0, 1))
-CROSS = (((3, 0), (3, 1), (3, 2), (3, 3), (2, 0), (2, 1), (2, 2), (2, 3)),
-         ((0, 0), (0, 1), (0, 2), (0, 3), (1, 0), (1, 1), (1, 2), (1, 3)))
-TAKE = ((0, 3, 2, 1), (1, 0, 3, 2), (2, 3, 0, 1), (3, 2, 0, 1))
 
 
 def loop(first, last, body):
@@ -54,7 +53,7 @@
 
 def kernel(n, blocks, fields, counts_in, owner_in, starts_in, weights_in, tm, series,
            data, counts, owner, starts, weights, start_row, weight_row, matrix, res, packed, arrived, wide,
-           load_sem, small_sem, send_sem, recv_sem, near, far, queued, again, queue_sem, again_sem, *lists):
+           load_sem, small_sem, send_sem, recv_sem, near, far, queued, again, queue_sem, again_sem, line, *lists):
     me = lax.axis_index("col")
     half = n // 2
     quarter = n // BANDS
@@ -76,6 +75,8 @@
         load.start()
         loads.append(load)
 
+    relayed = blocks <= 16 and quarter <= 16
+
     def greet(d):
         pl.semaphore_signal(
             barrier, inc=1, device_id={"col": d}, device_id_type=pl.DeviceIdType.MESH)
@@ -86,7 +87,10 @@
 
     @pl.when(band == 2)
     def _():
-        loop(0, quarter, lambda i: greet(quarter + i))
+        if relayed:
+            loop(0, quarter // 2, lambda i: greet(quarter + seat // (quarter // 2) * (quarter // 2) + i))
+        else:
+            loop(0, quarter, lambda i: greet(quarter + i))
         loop(0, quarter, lambda i: greet(half + quarter + i))
 
     @pl.when(band == 3)
@@ -106,7 +110,6 @@
         [weights[...], jnp.zeros((blocks * BAND, CBLK - PLEV), jnp.float32)], axis=1)
 
     unit = 1 << blocks.bit_length()
-    relayed = blocks <= 16 and quarter <= 16
     groups = -(-blocks // MOST)
 
     def third(x):
@@ -115,20 +118,54 @@
     def shift(c, turn):
         return jnp.where(c + turn >= MOST, c + turn - MOST, c + turn)
 
+    base = (1 - me // half) * half
+
+    def away(d):
+        return jnp.where(d < base, d - base + n, d - base)
+
     if relayed:
-        lower = jnp.int32(0)
-        for b in range(blocks):
-            lower = lower + jnp.where(owner[b] < half, 1, 0)
-
-    def before(d):
-        if not relayed:
-            return jnp.int32(0)
-        count = jnp.int32(0)
-        for b in range(blocks):
-            count = count + jnp.where(owner[b] < d, 1, 0)
-        return count - jnp.where(d >= half, lower, 0)
+        keys = [away(owner[b]) * unit + b for b in range(blocks)]
+        before = jnp.int32(0)
+        for key in keys:
+            before = before + jnp.where(key < half * unit, 1, 0)
+        size = 1 << (blocks - 1).bit_length()
+        ranked = keys + [jnp.int32(n * unit + blocks)] * (size - blocks)
+        p = 1
+        while p < size:
+            k = p
+            while k >= 1:
+                for j in range(k % p, size - k, 2 * k):
+                    for i in range(min(k, size - j - k)):
+                        if (i + j) // (2 * p) == (i + j + k) // (2 * p):
+                            x, y = ranked[i + j], ranked[i + j + k]
+                            ranked[i + j], ranked[i + j + k] = jnp.minimum(x, y), jnp.maximum(x, y)
+                k //= 2
+            p *= 2
+        ranked = ranked[:blocks]
+        for i in range(blocks):
+            line[i] = ranked[i]
+        for i in range(MOST):
+            line[blocks + i] = jnp.int32(n * unit + blocks)
+        queue = [key & (unit - 1) for key in ranked] + [jnp.int32(blocks)] * (groups * MOST - blocks)
+
+    def places(d):
+        first = jnp.int32(0)
+        for key in keys:
+            first = first + jnp.where(key < away(d) * unit, 1, 0)
+        listed = first - jnp.where(away(d) >= half, before, 0)
+        return first, listed, listed - MOST * third(listed)
+
+    def parts(d):
+        first, listed, turn = places(d)
+        for c in range(MOST):
+            step = jnp.where(c >= turn, c - turn, c - turn + MOST)
+            key = line[first + step]
+            yield key < (away(d) + 1) * unit, key & (unit - 1), listed + step
 
     def find(d):
+        if relayed:
+            return [jnp.where(mine, block, blocks) for mine, block, place in parts(d)]
+
         def look(i, found):
             b = blocks - 1 - i
             return jnp.where(owner[b] == d, found * unit + b, found)
@@ -141,55 +178,16 @@
                 found = look(i, found)
         else:
             found = lax.fori_loop(0, blocks, look, found)
-        found = [(found // unit ** s) % unit for s in range(MOST)]
-        if relayed:
-            first = before(d)
-            turn = first - MOST * third(first)
-            found = [
-                jnp.where(turn == 0, found[c], jnp.where(turn == 1, found[(c + 2) % 3], found[(c + 1) % 3]))
-                for c in range(MOST)
-            ]
-        return found
+        return [(found // unit ** s) % unit for s in range(MOST)]
 
     def locate(d):
-        first = before(d)
-        last = first
-        for b in range(blocks):
-            last = last + jnp.where(owner[b] == d, 1, 0)
-        turn = first - MOST * third(first)
-        where = []
-        for c in range(MOST):
-            place = first + jnp.where(c >= turn, c - turn, c - turn + MOST)
-            where.append(jnp.where(place < last, third(place), groups))
-        return where
-
-    def ordered(base):
-        keys = []
-        for b in range(blocks):
-            away = owner[b] - base
-            keys.append(jnp.where(away < 0, away + n, away) * unit + b)
-        size = 1 << (blocks - 1).bit_length()
-        keys += [jnp.int32(n * unit + blocks)] * (size - blocks)
-        p = 1
-        while p < size:
-            k = p
-            while k >= 1:
-                for j in range(k % p, size - k, 2 * k):
-                    for i in range(min(k, size - j - k)):
-                        if (i + j) // (2 * p) == (i + j + k) // (2 * p):
-                            x, y = keys[i + j], keys[i + j + k]
-                            keys[i + j], keys[i + j + k] = jnp.minimum(x, y), jnp.maximum(x, y)
-                k //= 2
-            p *= 2
-        keys = [key % unit for key in keys[:blocks]]
-        return keys + [jnp.int32(blocks)] * (groups * MOST - blocks)
+        return [jnp.where(mine, third(place), groups) for mine, block, place in parts(d)]
 
     def target(place, j):
         return choose(SEND, place, band) * quarter + ((seat + j) % quarter if place == OWN else j)
 
     early = None
     if relayed:
-        queue = ordered((1 - me // half) * half)
         inner = (band == 1) | (band == 2)
     elif quarter <= 16:
         early = [find(target(0, j)) for j in range(quarter)]
@@ -300,10 +298,14 @@
     for q in range(BANDS):
         @pl.when(band == q)
         def _(q=q):
-            pl.semaphore_wait(barrier, (2 * quarter - 1, 3 * quarter - 1, half, n - 1)[q])
+            pl.semaphore_wait(barrier, (
+                2 * quarter - 1, 2 * quarter - 1 + (quarter // 2 if relayed else quarter), half, n - 1)[q])
             if q == 1:
                 tell(near, me - quarter)
-                tell(near, me + quarter)
+                if relayed:
+                    tell(near, (seat + quarter // 2) % quarter)
+                else:
+                    tell(near, me + quarter)
             if q == 3:
                 for away in range(1, BANDS):
                     if not (relayed and away == 2):
@@ -364,12 +366,24 @@
         def _():
             for j in range(quarter):
                 pack(j, quarter + j)
-                if 0 < j <= EARLY:
+                if 0 < j <= EARLY[1]:
                     local(j - 1).start()
 
+            @pl.when(seat < quarter // 2)
+            def _():
+                for j in range(EARLY[1], EARLY[0]):
+                    local(j).start()
+
+        def slot_of(i):
+            return i if i < quarter else i + quarter
+
+        def spell(order):
+            return [p * quarter + a * quarter // 4 + i for p, a in order for i in range(quarter // 4)]
+
         @pl.when(band == 3)
         def _():
-            send_to(0, EDGE[1][0])
+            dests = spell(CROSS[1])
+            burst(len(dests), lambda i: pack(slot_of(i), dests[i]), lambda i: copy(slot_of(i), dests[i], me))
 
         @pl.when(inner)
         def _():
@@ -385,7 +399,6 @@
 
             @pl.when(band == 2)
             def _():
-                pl.semaphore_wait(near, 1)
                 pl.semaphore_wait(far, 1)
 
             send_to(0, jnp.where(band == 1, 0, 3))
@@ -398,18 +411,21 @@
 
         @pl.when(band == 0)
         def _():
-            pl.semaphore_wait(near, 1)
+            pl.semaphore_wait(near, 2)
             pl.semaphore_wait(far, 1)
-            for j in range(EARLY, quarter):
+
+            @pl.when(seat >= quarter // 2)
+            def _():
+                for j in range(EARLY[1], EARLY[0]):
+                    local(j).start()
+
+            for j in range(EARLY[0], quarter):
                 local(j).start()
+            dests = spell(CROSS[0])
+            burst(half, lambda i: pack(half + i, dests[i]), lambda i: copy(half + i, dests[i], me))
 
         @pl.when(jnp.logical_not(inner))
         def _():
-            cross = [jnp.where(band == 0, p * quarter + a, q * quarter + b)
-                     for (p, a), (q, b) in zip(*[
-                         [(p, a * quarter // 4 + i) for p, a in order for i in range(quarter // 4)]
-                         for order in CROSS])]
-            burst(half, lambda i: pack(half + i, cross[i]), lambda i: copy(half + i, cross[i], me))
             take_own()
 
             for place in range(1, BANDS):
@@ -509,8 +525,7 @@
         loop(0, OWN * quarter, sent)
         loop(OWN * quarter + 1, n, sent)
 
-    turn = before(me)
-    turn = turn - MOST * third(turn)
+    turn = places(me)[2] if relayed else jnp.int32(0)
     for s in range(MOST):
         series[s] = wide[pl.ds(shift(s, turn) * PLEV, PLEV)].astype(jnp.bfloat16)
 
@@ -564,6 +579,7 @@
             pltpu.VMEM((n // 2, ROWS, CBLK), jnp.bfloat16),
             pltpu.SemaphoreType.DMA((4 * STEPS,)),
             pltpu.SemaphoreType.DMA((n // 2,)),
+            pltpu.SMEM((blocks + MOST,), jnp.int32),
             *[pltpu.VMEM((min(last, -(-blocks // MOST)) + 1, ROWS, CBLK), jnp.bfloat16) for last in STAGES[1:]],
         ],
         compiler_params=pltpu.CompilerParams(

time: 15.3 us -> 15 us (0.980)
  Pallas kernels: 14.5 us -> 14.3 us
    pallas_call x1, Pallas kernels: 13.7 us -> 13.4 us  [per_device(): pl.pallas_call(functools.partial(kernel, n, blocks), out_shape=(jax.Shape...]
where the time goes in v4:
time: 15 us; the launch traced here: 14.9 us
  Pallas kernels  14.3 us (95%)
  between operations  0.64 us (4%)
    pallas_call x1, Pallas kernels, per_device(): pl.pallas_call(functools.partial(kernel, n, blocks), out_shape=(jax.Shape...  13.4 us
    pallas_call x1, Pallas kernels, per_device(): pl.pallas_call(close, out_shape=(jax.ShapeDtypeStruct((1, PLEV, cols), jn...  0.84 us

profile of v4, /device:TPU:0, one launch (start us, length us, event | category | flops | bytes accessed | tf_op | source)
XLA Modules:
  0.0 14.9 jit_solution(14628770090734795826)
XLA Ops:
  0.6 13.4 %shard_map.68 = (bf16[1,37,2048]{2,1,0:T(8,128)(2,1)S(1)}, bf16[3,37,16,128]{3,2,1,0:T(8,128)(2,1)S(1)}) custom-call(bf16[1,137,2048]{2,1,0:T(8,128)(2,1)} %fields.1, s32[16,128]{1,0:T(8,128)} %bitcast.5, s32[16]{0:T(128)} %owner_in.1, s32[16,37]{1,0:T(8,128)} %starts_in.1, f32[64,37]{1,0:T(8,128)} %bitcast.4), custom_call_target="tpu_custom_call" | custom-call | tf_op jit(solution)/shard_map/pallas_call | solution.py:551
  14.1 0.8 %shard_map.69 = (bf16[1,37,2048]{2,1,0:T(8,128)(2,1)}, bf16[3,37,16,128]{3,2,1,0:T(8,128)(2,1)}) custom-call(bf16[1,37,2048]{2,1,0:T(8,128)(2,1)S(1)} %get-tuple-element.4.tm, bf16[3,37,16,128]{3,2,1,0:T(8,128)(2,1)S(1)} %get-tuple-element.5.series), custom_call_target="tpu_custom_call" | custom-call | tf_op jit(solution)/shard_map/pallas_call | solution.py:594

commit v5 on v4

--- a/solution.py
+++ b/solution.py
@@ -25,7 +25,7 @@
 OWN_AT = 1
 EARLY = (4, 3)
 CROSS = (((3, 0), (3, 1), (3, 2), (3, 3), (2, 0), (2, 1), (2, 2), (2, 3)),
-         ((2, 0), (2, 1), (2, 2), (0, 0), (2, 3), (0, 1), (0, 2), (1, 0), (0, 3), (1, 1), (1, 2), (1, 3)))
+         ((2, 0), (2, 1), (2, 2), (2, 3), (0, 0), (0, 1), (1, 0), (0, 2), (0, 3), (1, 1), (1, 2), (1, 3)))
 EDGE_TAKE = ((0, 1, 3, 2), (3, 2, 0, 1))
 STAGES = (0, 2, 4, 1 << 20)
 STEPS = len(STAGES) - 1
@@ -95,7 +95,11 @@
 
     @pl.when(band == 3)
     def _():
-        loop(1, quarter, lambda i: greet(half + quarter + (seat + i) % quarter))
+        if relayed:
+            part = seat // (quarter // 2) * (quarter // 2)
+            loop(1, quarter // 2, lambda i: greet(half + quarter + part + (seat + i) % (quarter // 2)))
+        else:
+            loop(1, quarter, lambda i: greet(half + quarter + (seat + i) % quarter))
 
     res[blocks] = jnp.zeros(res.shape[1:], jnp.bfloat16)
     for part in lists:
@@ -299,7 +303,8 @@
         @pl.when(band == q)
         def _(q=q):
             pl.semaphore_wait(barrier, (
-                2 * quarter - 1, 2 * quarter - 1 + (quarter // 2 if relayed else quarter), half, n - 1)[q])
+                2 * quarter - 1, 2 * quarter - 1 + (quarter // 2 if relayed else quarter), half,
+                n - 1 - (quarter // 2 if relayed else 0))[q])
             if q == 1:
                 tell(near, me - quarter)
                 if relayed:
@@ -307,9 +312,13 @@
                 else:
                     tell(near, me + quarter)
             if q == 3:
-                for away in range(1, BANDS):
-                    if not (relayed and away == 2):
-                        tell(far, me - away * quarter)
+                if relayed:
+                    for first in (0, half):
+                        tell(far, first + seat)
+                        tell(far, first + (seat + quarter // 2) % quarter)
+                else:
+                    for step in range(1, BANDS):
+                        tell(far, me - step * quarter)
 
     def spread(t, rows):
         wide[:, pl.ds(t, 1), :] = rows.astype(jnp.float32)[:, None, :]
@@ -384,6 +393,7 @@
         def _():
             dests = spell(CROSS[1])
             burst(len(dests), lambda i: pack(slot_of(i), dests[i]), lambda i: copy(slot_of(i), dests[i], me))
+            pl.semaphore_wait(near, 1)
 
         @pl.when(inner)
         def _():
@@ -399,7 +409,8 @@
 
             @pl.when(band == 2)
             def _():
-                pl.semaphore_wait(far, 1)
+                pl.semaphore_wait(far, 2)
+                tell(near, me + quarter)
 
             send_to(0, jnp.where(band == 1, 0, 3))
 
@@ -412,7 +423,7 @@
         @pl.when(band == 0)
         def _():
             pl.semaphore_wait(near, 2)
-            pl.semaphore_wait(far, 1)
+            pl.semaphore_wait(far, 2)
 
             @pl.when(seat >= quarter // 2)
             def _():

time: 15 us -> 14.9 us (level)
  the two profiles are of different devices: /device:TPU:0 before, /device:TPU:9 now
where the time goes in v5:
time: 14.9 us; the launch traced here: 14.7 us
  Pallas kernels  14.1 us (95%)
  between operations  0.64 us (4%)
    pallas_call x1, Pallas kernels, per_device(): pl.pallas_call(functools.partial(kernel, n, blocks), out_shape=(jax.Shape...  13.3 us
    pallas_call x1, Pallas kernels, per_device(): pl.pallas_call(close, out_shape=(jax.ShapeDtypeStruct((1, PLEV, cols), jn...  0.84 us

profile of v5, /device:TPU:9, one launch (start us, length us, event | category | flops | bytes accessed | tf_op | source)
XLA Modules:
  0.0 14.7 jit_solution(15070345656104705989)
XLA Ops:
  0.6 13.3 %shard_map.68 = (bf16[1,37,2048]{2,1,0:T(8,128)(2,1)S(1)}, bf16[3,37,16,128]{3,2,1,0:T(8,128)(2,1)S(1)}) custom-call(bf16[1,137,2048]{2,1,0:T(8,128)(2,1)} %fields.1, s32[16,128]{1,0:T(8,128)} %bitcast.5, s32[16]{0:T(128)} %owner_in.1, s32[16,37]{1,0:T(8,128)} %starts_in.1, f32[64,37]{1,0:T(8,128)} %bitcast.4), custom_call_target="tpu_custom_call" | custom-call | tf_op jit(solution)/shard_map/pallas_call | solution.py:562
  13.9 0.8 %shard_map.69 = (bf16[1,37,2048]{2,1,0:T(8,128)(2,1)}, bf16[3,37,16,128]{3,2,1,0:T(8,128)(2,1)}) custom-call(bf16[1,37,2048]{2,1,0:T(8,128)(2,1)S(1)} %get-tuple-element.4.tm, bf16[3,37,16,128]{3,2,1,0:T(8,128)(2,1)S(1)} %get-tuple-element.5.series), custom_call_target="tpu_custom_call" | custom-call | tf_op jit(solution)/shard_map/pallas_call | solution.py:605

commit v6 on v5

--- a/solution.py
+++ b/solution.py
@@ -387,7 +387,9 @@
             return i if i < quarter else i + quarter
 
         def spell(order):
-            return [p * quarter + a * quarter // 4 + i for p, a in order for i in range(quarter // 4)]
+            swap = (me % 2) * (quarter // 4)
+            return [p * quarter + a * quarter // 4 + i + swap * (1 - 2 * (a % 2))
+                    for p, a in order for i in range(quarter // 4)]
 
         @pl.when(band == 3)
         def _():

time: 14.9 us -> 14.9 us (level)
  no operation moved by 1% of the time
where the time goes in v6:
time: 14.9 us; the launch traced here: 14.8 us
  Pallas kernels  14.1 us (95%)
  between operations  0.64 us (4%)
    pallas_call x1, Pallas kernels, per_device(): pl.pallas_call(functools.partial(kernel, n, blocks), out_shape=(jax.Shape...  13.3 us
    pallas_call x1, Pallas kernels, per_device(): pl.pallas_call(close, out_shape=(jax.ShapeDtypeStruct((1, PLEV, cols), jn...  0.84 us

profile of v6, /device:TPU:9, one launch (start us, length us, event | category | flops | bytes accessed | tf_op | source)
XLA Modules:
  0.0 14.8 jit_solution(8465652446119839635)
XLA Ops:
  0.6 13.3 %shard_map.68 = (bf16[1,37,2048]{2,1,0:T(8,128)(2,1)S(1)}, bf16[3,37,16,128]{3,2,1,0:T(8,128)(2,1)S(1)}) custom-call(bf16[1,137,2048]{2,1,0:T(8,128)(2,1)} %fields.1, s32[16,128]{1,0:T(8,128)} %bitcast.5, s32[16]{0:T(128)} %owner_in.1, s32[16,37]{1,0:T(8,128)} %starts_in.1, f32[64,37]{1,0:T(8,128)} %bitcast.4), custom_call_target="tpu_custom_call" | custom-call | tf_op jit(solution)/shard_map/pallas_call | solution.py:564
  13.9 0.8 %shard_map.69 = (bf16[1,37,2048]{2,1,0:T(8,128)(2,1)}, bf16[3,37,16,128]{3,2,1,0:T(8,128)(2,1)}) custom-call(bf16[1,37,2048]{2,1,0:T(8,128)(2,1)S(1)} %get-tuple-element.4.tm, bf16[3,37,16,128]{3,2,1,0:T(8,128)(2,1)S(1)} %get-tuple-element.5.series), custom_call_target="tpu_custom_call" | custom-call | tf_op jit(solution)/shard_map/pallas_call | solution.py:607
